TPU v7x, 32 devices: a whole 2x2x4 slice. The times are simulated.
32 devices in a mesh: space: 8 (over z, y), tm: 4 (over x, core).
Axes of the slice: x: 2, y: 2, z: 4, core: 2. Of those that a mesh axis runs over, the one named last changes fastest.
Arguments:
- precip: float32 [512, 48, 2048], P('tm', 'space'), may hold values from 0.0001 to 0.01
Outputs:
- totals: float32 [48, 2048, 512], P(None, 'space', 'tm')
All inputs are finite; a program needn't handle non-finite values.
Results may differ from a plain program's by a relative error of at most 0.00005.
Values sent between devices are 32-bit elements; how exact they have to be, the bound alone decides.
A program may use at most 64 MiB of HBM per device.

v0:
```python
import jax
import jax.numpy as jnp
from jax import lax
from jax.sharding import PartitionSpec as P


def entering(part, axis, combine, identity):
    place = lax.axis_index(axis)
    gathered = lax.all_gather(part, axis)
    state = jnp.zeros_like(part) + jnp.asarray(identity, part.dtype)

    def one(turn, state):
        return combine(state, lax.dynamic_index_in_dim(gathered, turn, 0, False))

    return lax.fori_loop(0, place, one, state)


def rechunk(source):
    return lax.all_to_all(source, "space", split_axis=2, concat_axis=1, tiled=True)


def add_terms(earlier_part, later_part):
    return earlier_part + later_part


def day_prefix(pixel_major, upper_ones):
    lat_rows, lon_cols, day_count = pixel_major.shape
    flat_rows = pixel_major.reshape(lat_rows * lon_cols, day_count)
    summed = jnp.dot(
        flat_rows, upper_ones, precision=lax.Precision.HIGHEST, preferred_element_type=jnp.float32
    )
    return summed.reshape(lat_rows, lon_cols, day_count)


def per_device(precip):
    day_count = precip.shape[0]
    position = lax.broadcasted_iota(jnp.int32, (day_count, day_count), 0)
    later_pos = lax.broadcasted_iota(jnp.int32, (day_count, day_count), 1)
    upper_ones = (position <= later_pos).astype(jnp.float32)
    pixel_major = jnp.transpose(rechunk(precip), (1, 2, 0))
    running = day_prefix(pixel_major, upper_ones)
    last_day = running[:, :, -1]
    carried = entering(last_day, "tm", add_terms, jnp.zeros_like(last_day))
    return running + carried[:, :, None]


def solution(mesh):
    return jax.shard_map(
        per_device,
        mesh=mesh,
        in_specs=(P("tm", "space", None),),
        out_specs=P(None, "space", "tm"),
        check_vma=False,
    )
```

profile of v0, /device:TPU:0, one launch (start us, length us, event | category | flops | bytes accessed | tf_op | source)
XLA Modules:
  0.0 231.7 jit_solution(16729160938471448487)
XLA Ops:
  0.0 8.4 %copy.8 = f32[128,6,2048]{0,1,2:T(8,128)} copy(f32[128,6,2048]{2,0,1:T(8,128)} %param.3) | data formatting | bytes 12582912 | tf_op args[0]
  8.4 7.3 %all-to-all-start = ((f32[128,6,2048]{0,1,2:T(8,128)}), f32[128,6,2048]{0,1,2:T(8,128)}, u32[]{:S(2)}, u32[]{:S(2)}) async-start(f32[128,6,2048]{0,1,2:T(8,128)} %copy.8), calls=%async_computation | async-start | bytes 16777216 | tf_op jit(solution)/shard_map/all_to_all | solution.py:19
  15.7 183.2 %all-to-all-done = f32[128,6,2048]{0,1,2:T(8,128)} async-done(((f32[128,6,2048]{0,1,2:T(8,128)}), f32[128,6,2048]{0,1,2:T(8,128)}, u32[]{:S(2)}, u32[]{:S(2)}) %all-to-all-start) | async-done | bytes 6291488 | tf_op jit(solution)/shard_map/all_to_all | solution.py:19
  198.9 4.5 %copy.14 = f32[128,8,6,256]{0,3,2,1:T(8,128)S(1)} copy(f32[128,8,6,256]{0,2,3,1:T(8,128)} %bitcast.3) | data formatting | bytes 12582912 | tf_op jit(solution)/shard_map/transpose | solution.py:40
  203.4 3.3 %fusion.1 = f32[128,12288]{1,0:T(8,128)S(1)} fusion(f32[12288,128]{1,0:T(8,128)S(1)} %bitcast.21), kind=kOutput, calls=%fused_computation.4 | convolution fusion | flops 2415951872 | bytes 12582912 | tf_op jit(solution)/shard_map/dot_general | solution.py:29
  206.7 4.7 %copy.15 = f32[16,8,48,256]{3,2,1,0:T(8,128)} copy(f32[16,8,48,256]{3,1,2,0:T(8,128)S(1)} %bitcast.22) | data formatting | bytes 12582912
  211.3 6.7 %copy.12 = f32[48,256,128]{2,1,0:T(8,128)} copy(f32[48,256,128]{1,0,2:T(8,128)} %bitcast.19) | data formatting | bytes 12582912 | tf_op jit(solution)/shard_map/reshape | solution.py:32
  218.0 0.8 slice.4
  218.8 5.6 %all-gather = f32[192,256,1]{1,0,2:T(8,128)S(1)} all-gather(f32[48,256,1]{1,0,2:T(8,128)S(1)} %slice.4), channel_id=2, replica_groups=mesh['space'=8,'tm'=4] {'tm'}, dimensions={0}, use_global_device_ids=true | all-gather | bytes 245760 | tf_op jit(solution)/shard_map/all_gather | solution.py:9
  224.4 7.2 %broadcast_add_fusion = f32[48,256,128]{2,1,0:T(8,128)} fusion(f32[48,256,128]{2,1,0:T(8,128)} %copy.12, f32[48,256]{1,0:T(8,128)S(1)} %get-tuple-element.28), kind=kLoop, calls=%fused_computation.1 | loop fusion | flops 1572864 | bytes 12632064 | tf_op jit(solution)/shard_map/add | solution.py:44
  (2 shorter events, 0.0 us)
Async XLA Ops:
  8.4 190.5 %all-to-all-start = ((f32[128,6,2048]{0,1,2:T(8,128)}), f32[128,6,2048]{0,1,2:T(8,128)}, u32[]{:S(2)}, u32[]{:S(2)}) async-start(f32[128,6,2048]{0,1,2:T(8,128)} %copy.8), calls=%async_computation | async-start | bytes 16777216 | tf_op jit(solution)/shard_map/all_to_all | solution.py:19
where the time goes:
time: 232 us
  waiting for transfers between devices  183 us (79%)
  local copies, waits for them, and re-layouts  25 us (11%)
  starting transfers between devices  7.31 us (3%)
  other arithmetic  7.24 us (3%)
  blocking collectives  5.58 us (2%)
  matrix products  3.3 us (1%)
    all_to_all x1, waiting for transfers between devices, rechunk(): lax.all_to_all(source, 'space', split_axis=2, concat_axis=1, tiled=True)  183 us
    unnamed x2, local copies, waits for them, and re-layouts  13.1 us
    all_to_all x1, starting transfers between devices, rechunk(): lax.all_to_all(source, 'space', split_axis=2, concat_axis=1, tiled=True)  7.31 us
    add x1, other arithmetic, per_device(): return running + carried[:, :, None]  7.24 us
    reshape x1, local copies, waits for them, and re-layouts, day_prefix(): return summed.reshape(lat_rows, lon_cols, day_count)  6.69 us
    all_gather x1, blocking collectives, entering(): gathered = lax.all_gather(part, axis)  5.58 us
  transfers between devices with their start and end apart: 1, of which 1 were waited for; matrix products, arithmetic and copies ran while one was open for 0% of the time, Pallas kernels for 0%

commit v1 on v0

--- a/solution.py
+++ b/solution.py
@@ -2,6 +2,12 @@
 import jax.numpy as jnp
 from jax import lax
 from jax.sharding import PartitionSpec as P
+
+
+def swap_blocks(x, axis, split, join):
+    pieces = jnp.split(x, lax.axis_size(axis), axis=split)
+    arrived = lax.all_to_all(jnp.stack(pieces), axis, 0, 0)
+    return jnp.concatenate(arrived, axis=join)
 
 
 def entering(part, axis, combine, identity):
@@ -16,7 +22,7 @@
 
 
 def rechunk(source):
-    return lax.all_to_all(source, "space", split_axis=2, concat_axis=1, tiled=True)
+    return swap_blocks(source, "space", 2, 1)
 
 
 def add_terms(earlier_part, later_part):

time: 232 us -> 197 us (0.85)
  waiting for transfers between devices: 183 us -> 138 us
  local copies, waits for them, and re-layouts: 25 us -> 32.6 us
  matrix products: 3.3 us -> 6.29 us
    all_to_all x1, waiting for transfers between devices: 183 us -> 138 us  [swap_blocks(): arrived = lax.all_to_all(jnp.stack(pieces), axis, 0, 0)]
    add x0 -> x1, local copies, waits for them, and re-layouts: none -> 6.55 us  [per_device(): return running + carried[:, :, None]]
    transpose x1 -> x0, local copies, waits for them, and re-layouts: 4.5 us -> none  [per_device(): pixel_major = jnp.transpose(rechunk(precip), (1, 2, 0))]
    unnamed x2 -> x10, local copies, waits for them, and re-layouts: 13.1 us -> 17.4 us
    dot_general x1, matrix products: 3.3 us -> 6.29 us  [day_prefix(): jnp.dot(flat_rows, upper_ones, precision=lax.Precision.HIGHEST, preferred...]
where the time goes in v1:
time: 197 us
  waiting for transfers between devices  138 us (70%)
  local copies, waits for them, and re-layouts  32.6 us (17%)
  starting transfers between devices  7.31 us (4%)
  other arithmetic  6.66 us (3%)
  matrix products  6.29 us (3%)
  blocking collectives  5.6 us (3%)
    all_to_all x1, waiting for transfers between devices, swap_blocks(): arrived = lax.all_to_all(jnp.stack(pieces), axis, 0, 0)  138 us
    unnamed x10, local copies, waits for them, and re-layouts  17.4 us
    all_to_all x1, starting transfers between devices, swap_blocks(): arrived = lax.all_to_all(jnp.stack(pieces), axis, 0, 0)  7.31 us
    add x1, other arithmetic, per_device(): return running + carried[:, :, None]  6.66 us
    reshape x1, local copies, waits for them, and re-layouts, swap_blocks(): return jnp.concatenate(arrived, axis=join)  6.55 us
    add x1, local copies, waits for them, and re-layouts, per_device(): return running + carried[:, :, None]  6.55 us
    dot_general x1, matrix products, day_prefix(): jnp.dot(flat_rows, upper_ones, precision=lax.Precision.HIGHEST, preferred...  6.29 us
    all_gather x1, blocking collectives, entering(): gathered = lax.all_gather(part, axis)  5.6 us
  transfers between devices with their start and end apart: 1, of which 1 were waited for; matrix products, arithmetic and copies ran while one was open for 0% of the time, Pallas kernels for 0%

profile of v1, /device:TPU:0, one launch (start us, length us, event | category | flops | bytes accessed | tf_op | source)
XLA Modules:
  0.0 196.8 jit_solution(10137044305256790408)
XLA Ops:
  0.0 2.1 %bitcast_dynamic-update-slice_fusion.7 = f32[8,128,6,256]{3,1,2,0:T(8,128)} fusion(f32[128,6,2048]{2,0,1:T(8,128)} %param.3), kind=kLoop, calls=%fused_computation.9 | loop fusion | bytes 1572864
  2.1 2.1 %bitcast_dynamic-update-slice_fusion.6 = f32[8,128,6,256]{3,1,2,0:T(8,128)} fusion(f32[8,128,6,256]{3,1,2,0:T(8,128)} %bitcast_dynamic-update-slice_fusion.7, f32[128,6,2048]{2,0,1:T(8,128)} %param.3), kind=kLoop, calls=%fused_computation.8 | loop fusion | bytes 1572864
  4.2 2.1 %bitcast_dynamic-update-slice_fusion.5 = f32[8,128,6,256]{3,1,2,0:T(8,128)} fusion(f32[8,128,6,256]{3,1,2,0:T(8,128)} %bitcast_dynamic-update-slice_fusion.6, f32[128,6,2048]{2,0,1:T(8,128)} %param.3), kind=kLoop, calls=%fused_computation.7 | loop fusion | bytes 1572864
  6.3 2.1 %bitcast_dynamic-update-slice_fusion.4 = f32[8,128,6,256]{3,1,2,0:T(8,128)} fusion(f32[8,128,6,256]{3,1,2,0:T(8,128)} %bitcast_dynamic-update-slice_fusion.5, f32[128,6,2048]{2,0,1:T(8,128)} %param.3), kind=kLoop, calls=%fused_computation.6 | loop fusion | bytes 1572864
  8.4 2.1 %bitcast_dynamic-update-slice_fusion.3 = f32[8,128,6,256]{3,1,2,0:T(8,128)} fusion(f32[8,128,6,256]{3,1,2,0:T(8,128)} %bitcast_dynamic-update-slice_fusion.4, f32[128,6,2048]{2,0,1:T(8,128)} %param.3), kind=kLoop, calls=%fused_computation.5 | loop fusion | bytes 1572864
  10.5 2.1 %bitcast_dynamic-update-slice_fusion.2 = f32[8,128,6,256]{3,1,2,0:T(8,128)} fusion(f32[8,128,6,256]{3,1,2,0:T(8,128)} %bitcast_dynamic-update-slice_fusion.3, f32[128,6,2048]{2,0,1:T(8,128)} %param.3), kind=kLoop, calls=%fused_computation.4 | loop fusion | bytes 1572864
  12.6 2.1 %bitcast_dynamic-update-slice_fusion.1 = f32[8,128,6,256]{3,1,2,0:T(8,128)} fusion(f32[8,128,6,256]{3,1,2,0:T(8,128)} %bitcast_dynamic-update-slice_fusion.2, f32[128,6,2048]{2,0,1:T(8,128)} %param.3), kind=kLoop, calls=%fused_computation.3 | loop fusion | bytes 1572864
  14.7 2.1 %bitcast_dynamic-update-slice_fusion = f32[8,128,6,256]{3,1,2,0:T(8,128)} fusion(f32[8,128,6,256]{3,1,2,0:T(8,128)} %bitcast_dynamic-update-slice_fusion.1, f32[128,6,2048]{2,0,1:T(8,128)} %param.3), kind=kLoop, calls=%fused_computation.2 | loop fusion | bytes 1572864 | tf_op jit(solution)/shard_map/stack | solution.py:9
  16.8 7.3 %all-to-all-start = ((f32[8,128,6,256]{3,1,2,0:T(8,128)}), f32[8,128,6,256]{3,1,2,0:T(8,128)}, u32[]{:S(2)}, u32[]{:S(2)}) async-start(f32[8,128,6,256]{3,1,2,0:T(8,128)} %bitcast_dynamic-update-slice_fusion), calls=%async_computation | async-start | bytes 12582912 | tf_op jit(solution)/shard_map/all_to_all | solution.py:9
  24.1 138.2 %all-to-all-done = f32[8,128,6,256]{3,1,2,0:T(8,128)} async-done(((f32[8,128,6,256]{3,1,2,0:T(8,128)}), f32[8,128,6,256]{3,1,2,0:T(8,128)}, u32[]{:S(2)}, u32[]{:S(2)}) %all-to-all-start) | async-done | bytes 6291488 | tf_op jit(solution)/shard_map/all_to_all | solution.py:9
  162.3 6.6 %copy.4 = f32[128,8,6,256]{0,3,2,1:T(8,128)} copy(f32[128,8,6,256]{3,0,2,1:T(8,128)} %bitcast.9) | data formatting | bytes 12582912 | tf_op jit(solution)/shard_map/reshape | solution.py:10
  168.9 6.3 %fusion.1 = f32[48,256,128]{1,2,0:T(8,128)S(1)} fusion(f32[48,256,128]{2,1,0:T(8,128)} %bitcast.29), kind=kOutput, calls=%fused_computation.12 | convolution fusion | flops 2415935488 | bytes 12582912 | tf_op jit(solution)/shard_map/dot_general | solution.py:35
  175.2 0.0 copy-start
  175.2 2.7 %copy-done = f32[48,256,128]{1,2,0:T(8,128)} copy-done((f32[48,256,128]{1,2,0:T(8,128)}, f32[48,256,128]{1,2,0:T(8,128)S(1)}, u32[]{:S(2)}) %copy-start) | copy-done | bytes 6291480
  177.9 0.1 slice.4
  177.9 5.6 %all-gather = f32[192,256,1]{1,2,0:T(1,128)S(1)} all-gather(f32[48,256,1]{1,2,0:T(1,128)S(1)} %slice.4), channel_id=2, replica_groups=mesh['space'=8,'tm'=4] {'tm'}, dimensions={0}, use_global_device_ids=true | all-gather | bytes 245760 | tf_op jit(solution)/shard_map/all_gather | solution.py:15
  183.6 6.7 %broadcast_add_fusion = f32[48,256,128]{1,2,0:T(8,128)} fusion(f32[48,256,128]{1,2,0:T(8,128)} %copy-done, f32[48,256]{1,0:T(8,128)S(1)} %get-tuple-element.28), kind=kLoop, calls=%fused_computation.1 | loop fusion | flops 1572864 | bytes 12632064 | tf_op jit(solution)/shard_map/add | solution.py:50
  190.2 6.6 %copy.5 = f32[48,256,128]{2,1,0:T(8,128)} copy(f32[48,256,128]{1,2,0:T(8,128)} %broadcast_add_fusion) | data formatting | bytes 12582912 | tf_op jit(solution)/shard_map/add | solution.py:50
  (3 shorter events, 0.0 us)
Async XLA Ops:
  16.8 145.5 %all-to-all-start = ((f32[8,128,6,256]{3,1,2,0:T(8,128)}), f32[8,128,6,256]{3,1,2,0:T(8,128)}, u32[]{:S(2)}, u32[]{:S(2)}) async-start(f32[8,128,6,256]{3,1,2,0:T(8,128)} %bitcast_dynamic-update-slice_fusion), calls=%async_computation | async-start | bytes 12582912 | tf_op jit(solution)/shard_map/all_to_all | solution.py:9
  175.2 2.7 %copy-start = (f32[48,256,128]{1,2,0:T(8,128)}, f32[48,256,128]{1,2,0:T(8,128)S(1)}, u32[]{:S(2)}) copy-start(f32[48,256,128]{1,2,0:T(8,128)S(1)} %fusion.1) | copy-start | bytes 18874372
